TPU v7x, 32 devices: a whole 2x2x4 slice. The times are simulated.
32 devices in a mesh: row: 2 (over x), col: 16 (over z, y, core).
Axes of the slice: x: 2, y: 2, z: 4, core: 2. Of those that a mesh axis runs over, the one named last changes fastest.
Arguments:
- adjacency: int32 [2048, 64], P('row', 'col'), may hold values from -2147483648 to 2147483647, as said below
- tile_mask: int32 [16, 16], P('row', 'col'), may hold values from 0 to 1, as said below
- thresholds: int32 [3], replicated, may hold values from 30 to 61
Outputs:
- truss_support: float32 [2048, 2048], P('row', 'col')
- edge_counts: int32 [3], replicated
Inputs may be any that keep to these rules, and one draw needn't show every extreme that they name: The graph of adjacency is symmetric with an empty diagonal: bit b of word w of row i equals the bit for row 32 w + b and column i. `tile_mask`: Symmetric.
All inputs are finite; a program needn't handle non-finite values.
Results may differ from a plain program's by a relative error of at most 0.0003.
Values may be sent and summed in bfloat16 or wider, within the bound.
No kernel may reach another device: no remote copies, remote signals or barrier semaphores. Data moves between devices by JAX's collectives and lax.ppermute only.
A program may use at most 64 MiB of HBM per device.

v0:
```python
import jax
import jax.numpy as jnp
from jax import lax
from jax.sharding import PartitionSpec as P

TILE = 128
ITERS = 3


def unpack_bits(packed_rows):
    shifts = jnp.arange(32, dtype=jnp.int32)
    flat_bits = jnp.bitwise_and(jnp.right_shift(packed_rows[:, :, None], shifts), 1)
    return flat_bits.reshape(packed_rows.shape[0], packed_rows.shape[1] * 32)


def pack_bits(flat_bits):
    shifts = jnp.arange(32, dtype=jnp.int32)
    grouped = flat_bits.reshape(flat_bits.shape[0], flat_bits.shape[1] // 32, 32)
    return jnp.sum(jnp.left_shift(grouped, shifts), axis=-1, dtype=jnp.int32)


def block_product(packed_rows, matching):
    operand = unpack_bits(packed_rows).astype(jnp.bfloat16)
    return jnp.dot(operand, matching, preferred_element_type=jnp.float32)


def local(adjacency, tile_mask, thresholds):
    rows_here = adjacency.shape[0]
    cols_here = adjacency.shape[1] * 32
    flat_bits = unpack_bits(adjacency)
    tile_cover = jnp.broadcast_to(
        tile_mask[:, None, :, None], (tile_mask.shape[0], TILE, tile_mask.shape[1], TILE)
    )
    surviving = flat_bits * tile_cover.reshape(rows_here, cols_here)
    survived_list = []
    support = jnp.zeros((rows_here, cols_here), jnp.float32)
    for iteration in range(ITERS):
        packed_here = pack_bits(surviving)
        column_words = lax.all_gather(packed_here, "row", axis=0, tiled=True)
        column_bits = unpack_bits(column_words)
        lower_panel = column_bits.astype(jnp.bfloat16)
        wedge_counts = block_product(
            lax.all_gather(packed_here, "col", axis=1, tiled=True), lower_panel
        )
        support = wedge_counts * surviving.astype(jnp.float32)
        retained = (support >= thresholds[iteration].astype(jnp.float32)).astype(jnp.int32)
        surviving = surviving * retained
        survived = jnp.sum(surviving)
        survived_list.append(survived)
    edge_counts = lax.psum(jnp.stack(survived_list), ("row", "col"))
    truss_support = (
        support * surviving.astype(jnp.float32) / thresholds[ITERS - 1].astype(jnp.float32)
    )
    return (truss_support, edge_counts)


def solution(mesh):
    in_specs = (P("row", "col"), P("row", "col"), P())
    out_specs = (P("row", "col"), P())
    return jax.shard_map(local, mesh=mesh, in_specs=in_specs, out_specs=out_specs, check_vma=False)
```

profile of v0, /device:TPU:14, one launch (start us, length us, event | category | flops | bytes accessed | tf_op | source)
XLA Modules:
  0.0 131.3 jit_solution(8113006497730622411)
XLA Ops:
  0.6 0.6 copy-done
  1.3 1.3 %fusion.8 = (s32[1]{0:T(128)}, s32[1]{0:T(128)}, s32[1]{0:T(128)}) fusion(s32[3]{0:T(128)} %param.5), kind=kLoop, calls=%fused_computation.25 | loop fusion | bytes 24 | tf_op jit(solution)/shard_map/slice | solution.py:46
  4.7 0.8 shift-left_reduce_fusion.2
  5.5 4.4 %all_gather.19 = s32[2048,4]{0,1:T(4,128)S(1)} all-gather(s32[1024,4]{0,1:T(4,128)S(1)} %shift-left_reduce_fusion.2), channel_id=1, replica_groups=mesh['row'=2,'col'=16] {'row'}, dimensions={0}, use_global_device_ids=true | all-gather | bytes 49152 | tf_op jit(solution)/shard_map/all_gather | solution.py:39
  9.9 15.8 %all-gather = s32[16,4,1024]{2,1,0:T(4,128)S(1)} all-gather(s32[1,4,1024]{2,1,0:T(4,128)S(1)} %bitcast.55), channel_id=1, replica_groups=mesh['row'=2,'col'=16] {'col'}, dimensions={0}, use_global_device_ids=true | all-gather | bytes 278528 | tf_op jit(solution)/shard_map/all_gather | solution.py:43
  25.8 0.1 and_convert_fusion.5
  26.0 0.8 fusion.5
  26.8 1.6 %and_convert_fusion.2 = bf16[1024,64,32]{0,2,1:T(8,128)(2,1)S(1)} fusion(s32[1024,64]{0,1:T(8,128)S(1)} %bitcast.49), kind=kLoop, calls=%fused_computation.2 | loop fusion | flops 6291456 | bytes 4456448 | tf_op jit(solution)/shard_map/convert_element_type | solution.py:23
  28.4 0.9 shift-left_reduce_fusion.1
  29.3 0.8 reduce_sum.57
  30.0 4.4 %all_gather.21 = s32[2048,4]{0,1:T(4,128)S(1)} all-gather(s32[1024,4]{0,1:T(4,128)S(1)} %get-tuple-element.13), channel_id=1, replica_groups=mesh['row'=2,'col'=16] {'row'}, dimensions={0}, use_global_device_ids=true | all-gather | bytes 49152 | tf_op jit(solution)/shard_map/all_gather | solution.py:39
  34.4 22.1 %all-gather.1 = s32[16,4,1024]{2,1,0:T(4,128)S(1)} all-gather(s32[1,4,1024]{2,1,0:T(4,128)S(1)} %bitcast.53), channel_id=1, replica_groups=mesh['row'=2,'col'=16] {'col'}, dimensions={0}, use_global_device_ids=true | all-gather | bytes 278528 | tf_op jit(solution)/shard_map/all_gather | solution.py:43
  56.6 0.1 and_convert_fusion.4
  56.8 1.6 %and_convert_fusion.1 = bf16[1024,64,32]{0,2,1:T(8,128)(2,1)S(1)} fusion(s32[1024,64]{0,1:T(8,128)S(1)} %bitcast.50), kind=kLoop, calls=%fused_computation.1 | loop fusion | flops 6291456 | bytes 4456448 | tf_op jit(solution)/shard_map/convert_element_type | solution.py:23
  58.3 0.9 shift-left_reduce_fusion
  59.3 4.4 %all_gather.23 = s32[2048,4]{0,1:T(4,128)S(1)} all-gather(s32[1024,4]{0,1:T(4,128)S(1)} %get-tuple-element.15), channel_id=1, replica_groups=mesh['row'=2,'col'=16] {'row'}, dimensions={0}, use_global_device_ids=true | all-gather | bytes 49152 | tf_op jit(solution)/shard_map/all_gather | solution.py:39
  63.7 17.7 %all-gather.2 = s32[16,4,1024]{2,1,0:T(4,128)S(1)} all-gather(s32[1,4,1024]{2,1,0:T(4,128)S(1)} %bitcast.54), channel_id=1, replica_groups=mesh['row'=2,'col'=16] {'col'}, dimensions={0}, use_global_device_ids=true | all-gather | bytes 278528 | tf_op jit(solution)/shard_map/all_gather | solution.py:43
  81.5 0.1 and_convert_fusion.3
  81.6 1.6 %and_convert_fusion = bf16[1024,64,32]{0,2,1:T(8,128)(2,1)S(1)} fusion(s32[1024,64]{0,1:T(8,128)S(1)} %bitcast.51), kind=kLoop, calls=%fused_computation | loop fusion | flops 6291456 | bytes 4456448 | tf_op jit(solution)/shard_map/convert_element_type | solution.py:23
  83.2 0.9 multiply_divide_fusion
  84.0 0.9 fusion.7
  84.9 2.0 %pad_add_fusion = s32[3]{0:T(128)S(1)} fusion(s32[1]{0:T(128)} %bitcast.25, s32[1]{0:T(128)} %bitcast.24, s32[1]{0:T(128)} %bitcast.23), kind=kLoop, calls=%fused_computation.23 | loop fusion | flops 6 | bytes 24 | tf_op jit(solution)/shard_map/stack | solution.py:50
  86.9 1.0 copy.11
  87.9 43.4 %psum.7 = s32[3]{0:T(128)} all-reduce(s32[3]{0:T(128)S(1)} %pad_add_fusion), channel_id=1, replica_groups=mesh['row'=2,'col'=16] {'row','col'}, use_global_device_ids=true, to_apply=%region_6.0 | all-reduce | flops 3 | bytes 24 | tf_op jit(solution)/shard_map/psum | solution.py:50
  (7 shorter events, 0.4 us)
Async XLA Ops:
  0.6 0.7 copy-start
where the time goes:
time: 132 us; the launch traced here: 131 us
  blocking collectives  112 us (85%)
  other arithmetic  10.3 us (8%)
  local copies, waits for them, and re-layouts  3.42 us (3%)
  matrix products  2.66 us (2%)
  between operations  2.59 us (2%)
    all_gather x3, blocking collectives, local(): lax.all_gather(packed_here, 'col', axis=1, tiled=True)  55.6 us
    psum x1, blocking collectives, local(): edge_counts = lax.psum(jnp.stack(survived_list), ('row', 'col'))  43.4 us
    all_gather x3, blocking collectives, local(): column_words = lax.all_gather(packed_here, 'row', axis=0, tiled=True)  13.2 us
    convert_element_type x3, other arithmetic, block_product(): operand = unpack_bits(packed_rows).astype(jnp.bfloat16)  4.67 us
    dot_general x3, matrix products, block_product(): return jnp.dot(operand, matching, preferred_element_type=jnp.float32)  2.66 us

commit v1 on v0

--- a/solution.py
+++ b/solution.py
@@ -39,9 +39,30 @@
         column_words = lax.all_gather(packed_here, "row", axis=0, tiled=True)
         column_bits = unpack_bits(column_words)
         lower_panel = column_bits.astype(jnp.bfloat16)
-        wedge_counts = block_product(
-            lax.all_gather(packed_here, "col", axis=1, tiled=True), lower_panel
-        )
+
+        def shape_slices(z):
+            which_axis = "col"
+            lower = lax.axis_size(which_axis)
+            small = lax.axis_index(which_axis)
+            after, big, z2 = (lower, small, z.shape[1])
+            u1, right_arr = (z, 1)
+            while right_arr < after:
+                u1 = jnp.concatenate(
+                    [
+                        u1,
+                        lax.ppermute(
+                            u1,
+                            which_axis,
+                            [(hop_no, (hop_no - right_arr) % after) for hop_no in range(after)],
+                        ),
+                    ],
+                    axis=1,
+                )
+                right_arr = 2 * right_arr
+            answer = jnp.roll(u1, big * z2, axis=1)
+            return answer
+
+        wedge_counts = block_product(shape_slices(packed_here), lower_panel)
         support = wedge_counts * surviving.astype(jnp.float32)
         retained = (support >= thresholds[iteration].astype(jnp.float32)).astype(jnp.int32)
         surviving = surviving * retained

time: 132 us -> 127 us (0.962)
  blocking collectives: 112 us -> 55 us
  starting transfers between devices: 0 us -> 26.1 us
  waiting for transfers between devices: 0 us -> 25.9 us
    all_gather x3 -> x0, blocking collectives: 55.6 us -> none  [local(): lax.all_gather(packed_here, 'col', axis=1, tiled=True)]
    ppermute x0 -> x12, starting transfers between devices: none -> 26.1 us  [shape_slices(): lax.ppermute(u1, which_axis, [(hop_no, (hop_no - right_arr) % after) for...]
    ppermute x0 -> x12, waiting for transfers between devices: none -> 25.9 us  [shape_slices(): lax.ppermute(u1, which_axis, [(hop_no, (hop_no - right_arr) % after) for...]
    psum x1, blocking collectives: 43.4 us -> 41.8 us  [local(): edge_counts = lax.psum(jnp.stack(survived_list), ('row', 'col'))]
  transfers between devices with their start and end apart: 0 -> 12, of which waited for: 0 -> 9; matrix products, arithmetic and copies ran while one was open for 0% -> 3% of each run, Pallas kernels for 0% -> 0%
where the time goes in v1:
time: 127 us
  blocking collectives  55 us (43%)
  starting transfers between devices  26.1 us (21%)
  waiting for transfers between devices  25.9 us (20%)
  other arithmetic  10.7 us (8%)
  local copies, waits for them, and re-layouts  3.35 us (3%)
  between operations  2.84 us (2%)
  matrix products  2.72 us (2%)
    psum x1, blocking collectives, local(): edge_counts = lax.psum(jnp.stack(survived_list), ('row', 'col'))  41.8 us
    ppermute x12, starting transfers between devices, shape_slices(): lax.ppermute(u1, which_axis, [(hop_no, (hop_no - right_arr) % after) for...  26.1 us
    ppermute x12, waiting for transfers between devices, shape_slices(): lax.ppermute(u1, which_axis, [(hop_no, (hop_no - right_arr) % after) for...  25.9 us
    all_gather x3, blocking collectives, local(): column_words = lax.all_gather(packed_here, 'row', axis=0, tiled=True)  13.2 us
    convert_element_type x3, other arithmetic, block_product(): operand = unpack_bits(packed_rows).astype(jnp.bfloat16)  4.67 us
    dot_general x3, matrix products, block_product(): return jnp.dot(operand, matching, preferred_element_type=jnp.float32)  2.72 us
  transfers between devices with their start and end apart: 12, of which 9 were waited for; matrix products, arithmetic and copies ran while one was open for 3% of the time, Pallas kernels for 0%

profile of v1, /device:TPU:14, one launch (start us, length us, event | category | flops | bytes accessed | tf_op | source)
XLA Modules:
  0.0 126.6 jit_solution(2455557141201165117)
XLA Ops:
  2.3 1.4 %collective-permute-done = s32[1024,4]{0,1:T(4,128)S(1)} collective-permute-done((s32[1024,4]{0,1:T(4,128)S(1)}, s32[1024,4]{0,1:T(4,128)S(1)}, u32[]{:S(2)}, u32[]{:S(2)}) %collective-permute-start) | collective-permute-done | bytes 16416 | tf_op jit(solution)/shard_map/ppermute | solution.py:53
  5.1 3.5 %collective-permute-done.1 = s32[1024,8]{0,1:T(8,128)S(1)} collective-permute-done((s32[1024,8]{0,1:T(8,128)S(1)}, s32[1024,8]{0,1:T(8,128)S(1)}, u32[]{:S(2)}, u32[]{:S(2)}) %collective-permute-start.1) | collective-permute-done | bytes 32800 | tf_op jit(solution)/shard_map/ppermute | solution.py:53
  8.6 1.8 %collective-permute-start.2 = (s32[1024,16]{0,1:T(8,128)S(1)}, s32[1024,16]{0,1:T(8,128)S(1)}, u32[]{:S(2)}, u32[]{:S(2)}) collective-permute-start(s32[1024,16]{0,1:T(8,128)S(1)} %pad_add_fusion.3), channel_id=1, source_target_pairs={{0,12},{1,13},{2,14},{3,15},{4,0},{5,1},{6,2},{7,3},{8,4},{9,5},{1... | collective-permute-start | bytes 196616 | tf_op jit(solution)/shard_map/ppermute | solution.py:53
  10.4 4.4 %all_gather.9 = s32[2048,4]{0,1:T(4,128)S(1)} all-gather(s32[1024,4]{0,1:T(4,128)S(1)} %shift-left_reduce_fusion.2), channel_id=1, replica_groups=mesh['row'=2,'col'=16] {'row'}, dimensions={0}, use_global_device_ids=true | all-gather | bytes 49152 | tf_op jit(solution)/shard_map/all_gather | solution.py:39
  14.8 4.4 %collective-permute-start.3 = (s32[1024,32]{0,1:T(8,128)S(1)}, s32[1024,32]{0,1:T(8,128)S(1)}, u32[]{:S(2)}, u32[]{:S(2)}) collective-permute-start(s32[1024,32]{0,1:T(8,128)S(1)} %pad_add_fusion), channel_id=1, source_target_pairs={{0,8},{1,9},{2,10},{3,11},{4,12},{5,13},{6,14},{7,15},{8,0},{9,1},... | collective-permute-start | bytes 393224 | tf_op jit(solution)/shard_map/ppermute | solution.py:53
  22.4 2.7 %collective-permute-done.3 = s32[1024,32]{0,1:T(8,128)S(1)} collective-permute-done((s32[1024,32]{0,1:T(8,128)S(1)}, s32[1024,32]{0,1:T(8,128)S(1)}, u32[]{:S(2)}, u32[]{:S(2)}) %collective-permute-start.3) | collective-permute-done | bytes 131104 | tf_op jit(solution)/shard_map/ppermute | solution.py:53
  25.2 1.6 %and_convert_fusion.2 = bf16[1024,64,32]{0,2,1:T(8,128)(2,1)S(1)} fusion(s32[1024,64]{0,1:T(8,128)S(1)} %fusion.9), kind=kLoop, calls=%fused_computation.2 | loop fusion | flops 6291456 | bytes 4456448 | tf_op jit(solution)/shard_map/convert_element_type | solution.py:23
  27.7 1.4 %collective-permute-done.4 = s32[1024,4]{0,1:T(4,128)S(1)} collective-permute-done((s32[1024,4]{0,1:T(4,128)S(1)}, s32[1024,4]{0,1:T(4,128)S(1)}, u32[]{:S(2)}, u32[]{:S(2)}) %collective-permute-start.4) | collective-permute-done | bytes 16416 | tf_op jit(solution)/shard_map/ppermute | solution.py:53
  29.2 3.9 %collective-permute-start.5 = (s32[1024,8]{0,1:T(8,128)S(1)}, s32[1024,8]{0,1:T(8,128)S(1)}, u32[]{:S(2)}, u32[]{:S(2)}) collective-permute-start(s32[1024,8]{0,1:T(8,128)S(1)} %pad_add_fusion.7), channel_id=1, source_target_pairs={{0,14},{1,15},{2,0},{3,1},{4,2},{5,3},{6,4},{7,5},{8,6},{9,7},{10,... | collective-permute-start | bytes 98312 | tf_op jit(solution)/shard_map/ppermute | solution.py:53
  33.1 1.6 %collective-permute-done.5 = s32[1024,8]{0,1:T(8,128)S(1)} collective-permute-done((s32[1024,8]{0,1:T(8,128)S(1)}, s32[1024,8]{0,1:T(8,128)S(1)}, u32[]{:S(2)}, u32[]{:S(2)}) %collective-permute-start.5) | collective-permute-done | bytes 32800 | tf_op jit(solution)/shard_map/ppermute | solution.py:53
  34.7 2.2 %collective-permute-start.6 = (s32[1024,16]{0,1:T(8,128)S(1)}, s32[1024,16]{0,1:T(8,128)S(1)}, u32[]{:S(2)}, u32[]{:S(2)}) collective-permute-start(s32[1024,16]{0,1:T(8,128)S(1)} %pad_add_fusion.4), channel_id=1, source_target_pairs={{0,12},{1,13},{2,14},{3,15},{4,0},{5,1},{6,2},{7,3},{8,4},{9,5},{1... | collective-permute-start | bytes 196616 | tf_op jit(solution)/shard_map/ppermute | solution.py:53
  37.6 4.4 %all_gather.10 = s32[2048,4]{0,1:T(4,128)S(1)} all-gather(s32[1024,4]{0,1:T(4,128)S(1)} %get-tuple-element.12), channel_id=1, replica_groups=mesh['row'=2,'col'=16] {'row'}, dimensions={0}, use_global_device_ids=true | all-gather | bytes 49152 | tf_op jit(solution)/shard_map/all_gather | solution.py:39
  42.0 3.4 %collective-permute-start.7 = (s32[1024,32]{0,1:T(8,128)S(1)}, s32[1024,32]{0,1:T(8,128)S(1)}, u32[]{:S(2)}, u32[]{:S(2)}) collective-permute-start(s32[1024,32]{0,1:T(8,128)S(1)} %pad_add_fusion.1), channel_id=1, source_target_pairs={{0,8},{1,9},{2,10},{3,11},{4,12},{5,13},{6,14},{7,15},{8,0},{9,1},... | collective-permute-start | bytes 393224 | tf_op jit(solution)/shard_map/ppermute | solution.py:53
  45.6 6.4 %collective-permute-done.7 = s32[1024,32]{0,1:T(8,128)S(1)} collective-permute-done((s32[1024,32]{0,1:T(8,128)S(1)}, s32[1024,32]{0,1:T(8,128)S(1)}, u32[]{:S(2)}, u32[]{:S(2)}) %collective-permute-start.7) | collective-permute-done | bytes 131104 | tf_op jit(solution)/shard_map/ppermute | solution.py:53
  52.1 1.6 %and_convert_fusion.1 = bf16[1024,64,32]{0,2,1:T(8,128)(2,1)S(1)} fusion(s32[1024,64]{0,1:T(8,128)S(1)} %fusion.8), kind=kLoop, calls=%fused_computation.1 | loop fusion | flops 6291456 | bytes 4456448 | tf_op jit(solution)/shard_map/convert_element_type | solution.py:23
  56.1 3.5 %collective-permute-start.9 = (s32[1024,8]{0,1:T(8,128)S(1)}, s32[1024,8]{0,1:T(8,128)S(1)}, u32[]{:S(2)}, u32[]{:S(2)}) collective-permute-start(s32[1024,8]{0,1:T(8,128)S(1)} %pad_add_fusion.8), channel_id=1, source_target_pairs={{0,14},{1,15},{2,0},{3,1},{4,2},{5,3},{6,4},{7,5},{8,6},{9,7},{10,... | collective-permute-start | bytes 98312 | tf_op jit(solution)/shard_map/ppermute | solution.py:53
  59.7 1.6 %collective-permute-done.9 = s32[1024,8]{0,1:T(8,128)S(1)} collective-permute-done((s32[1024,8]{0,1:T(8,128)S(1)}, s32[1024,8]{0,1:T(8,128)S(1)}, u32[]{:S(2)}, u32[]{:S(2)}) %collective-permute-start.9) | collective-permute-done | bytes 32800 | tf_op jit(solution)/shard_map/ppermute | solution.py:53
  61.3 2.6 %collective-permute-start.10 = (s32[1024,16]{0,1:T(8,128)S(1)}, s32[1024,16]{0,1:T(8,128)S(1)}, u32[]{:S(2)}, u32[]{:S(2)}) collective-permute-start(s32[1024,16]{0,1:T(8,128)S(1)} %pad_add_fusion.5), channel_id=1, source_target_pairs={{0,12},{1,13},{2,14},{3,15},{4,0},{5,1},{6,2},{7,3},{8,4},{9,5},{1... | collective-permute-start | bytes 196616 | tf_op jit(solution)/shard_map/ppermute | solution.py:53
  65.3 4.4 %all_gather.11 = s32[2048,4]{0,1:T(4,128)S(1)} all-gather(s32[1024,4]{0,1:T(4,128)S(1)} %get-tuple-element.14), channel_id=1, replica_groups=mesh['row'=2,'col'=16] {'row'}, dimensions={0}, use_global_device_ids=true | all-gather | bytes 49152 | tf_op jit(solution)/shard_map/all_gather | solution.py:39
  69.7 2.7 %collective-permute-start.11 = (s32[1024,32]{0,1:T(8,128)S(1)}, s32[1024,32]{0,1:T(8,128)S(1)}, u32[]{:S(2)}, u32[]{:S(2)}) collective-permute-start(s32[1024,32]{0,1:T(8,128)S(1)} %pad_add_fusion.2), channel_id=1, source_target_pairs={{0,8},{1,9},{2,10},{3,11},{4,12},{5,13},{6,14},{7,15},{8,0},{9,1},... | collective-permute-start | bytes 393224 | tf_op jit(solution)/shard_map/ppermute | solution.py:53
  72.5 5.8 %collective-permute-done.11 = s32[1024,32]{0,1:T(8,128)S(1)} collective-permute-done((s32[1024,32]{0,1:T(8,128)S(1)}, s32[1024,32]{0,1:T(8,128)S(1)}, u32[]{:S(2)}, u32[]{:S(2)}) %collective-permute-start.11) | collective-permute-done | bytes 131104 | tf_op jit(solution)/shard_map/ppermute | solution.py:53
  78.5 1.6 %and_convert_fusion = bf16[1024,64,32]{0,2,1:T(8,128)(2,1)S(1)} fusion(s32[1024,64]{0,1:T(8,128)S(1)} %fusion.7), kind=kLoop, calls=%fused_computation | loop fusion | flops 6291456 | bytes 4456448 | tf_op jit(solution)/shard_map/convert_element_type | solution.py:23
  81.8 2.0 %pad_add_fusion.9 = s32[3]{0:T(128)S(1)} fusion(s32[1]{0:T(128)} %bitcast.16, s32[1]{0:T(128)} %bitcast.15, s32[1]{0:T(128)} %bitcast.14), kind=kLoop, calls=%fused_computation.41 | loop fusion | flops 6 | bytes 24 | tf_op jit(solution)/shard_map/stack | solution.py:71
  84.8 41.8 %psum.7 = s32[3]{0:T(128)} all-reduce(s32[3]{0:T(128)S(1)} %pad_add_fusion.9), channel_id=1, replica_groups=mesh['row'=2,'col'=16] {'row','col'}, use_global_device_ids=true, to_apply=%region_6.8 | all-reduce | flops 3 | bytes 24 | tf_op jit(solution)/shard_map/psum | solution.py:71
  (40 shorter events, 13.1 us)
Async XLA Ops:
  0.6 0.7 copy-start
  2.2 1.5 %collective-permute-start = (s32[1024,4]{0,1:T(4,128)S(1)}, s32[1024,4]{0,1:T(4,128)S(1)}, u32[]{:S(2)}, u32[]{:S(2)}) collective-permute-start(s32[1024,4]{0,1:T(4,128)S(1)} %shift-left_reduce_fusion.2), channel_id=1, source_target_pairs={{0,15},{1,0},{2,1},{3,2},{4,3},{5,4},{6,5},{7,6},{8,7},{9,8},{10,9... | collective-permute-start | bytes 49160 | tf_op jit(solution)/shard_map/ppermute | solution.py:53
  3.7 4.9 %collective-permute-start.1 = (s32[1024,8]{0,1:T(8,128)S(1)}, s32[1024,8]{0,1:T(8,128)S(1)}, u32[]{:S(2)}, u32[]{:S(2)}) collective-permute-start(s32[1024,8]{0,1:T(8,128)S(1)} %pad_add_fusion.6), channel_id=1, source_target_pairs={{0,14},{1,15},{2,0},{3,1},{4,2},{5,3},{6,4},{7,5},{8,6},{9,7},{10,... | collective-permute-start | bytes 98312 | tf_op jit(solution)/shard_map/ppermute | solution.py:53
  8.6 6.2 %collective-permute-start.2 = (s32[1024,16]{0,1:T(8,128)S(1)}, s32[1024,16]{0,1:T(8,128)S(1)}, u32[]{:S(2)}, u32[]{:S(2)}) collective-permute-start(s32[1024,16]{0,1:T(8,128)S(1)} %pad_add_fusion.3), channel_id=1, source_target_pairs={{0,12},{1,13},{2,14},{3,15},{4,0},{5,1},{6,2},{7,3},{8,4},{9,5},{1... | collective-permute-start | bytes 196616 | tf_op jit(solution)/shard_map/ppermute | solution.py:53
  14.8 10.2 %collective-permute-start.3 = (s32[1024,32]{0,1:T(8,128)S(1)}, s32[1024,32]{0,1:T(8,128)S(1)}, u32[]{:S(2)}, u32[]{:S(2)}) collective-permute-start(s32[1024,32]{0,1:T(8,128)S(1)} %pad_add_fusion), channel_id=1, source_target_pairs={{0,8},{1,9},{2,10},{3,11},{4,12},{5,13},{6,14},{7,15},{8,0},{9,1},... | collective-permute-start | bytes 393224 | tf_op jit(solution)/shard_map/ppermute | solution.py:53
  27.7 1.5 %collective-permute-start.4 = (s32[1024,4]{0,1:T(4,128)S(1)}, s32[1024,4]{0,1:T(4,128)S(1)}, u32[]{:S(2)}, u32[]{:S(2)}) collective-permute-start(s32[1024,4]{0,1:T(4,128)S(1)} %get-tuple-element.12), channel_id=1, source_target_pairs={{0,15},{1,0},{2,1},{3,2},{4,3},{5,4},{6,5},{7,6},{8,7},{9,8},{10,9... | collective-permute-start | bytes 49160 | tf_op jit(solution)/shard_map/ppermute | solution.py:53
  29.2 5.5 %collective-permute-start.5 = (s32[1024,8]{0,1:T(8,128)S(1)}, s32[1024,8]{0,1:T(8,128)S(1)}, u32[]{:S(2)}, u32[]{:S(2)}) collective-permute-start(s32[1024,8]{0,1:T(8,128)S(1)} %pad_add_fusion.7), channel_id=1, source_target_pairs={{0,14},{1,15},{2,0},{3,1},{4,2},{5,3},{6,4},{7,5},{8,6},{9,7},{10,... | collective-permute-start | bytes 98312 | tf_op jit(solution)/shard_map/ppermute | solution.py:53
  34.7 7.3 %collective-permute-start.6 = (s32[1024,16]{0,1:T(8,128)S(1)}, s32[1024,16]{0,1:T(8,128)S(1)}, u32[]{:S(2)}, u32[]{:S(2)}) collective-permute-start(s32[1024,16]{0,1:T(8,128)S(1)} %pad_add_fusion.4), channel_id=1, source_target_pairs={{0,12},{1,13},{2,14},{3,15},{4,0},{5,1},{6,2},{7,3},{8,4},{9,5},{1... | collective-permute-start | bytes 196616 | tf_op jit(solution)/shard_map/ppermute | solution.py:53
  42.0 9.9 %collective-permute-start.7 = (s32[1024,32]{0,1:T(8,128)S(1)}, s32[1024,32]{0,1:T(8,128)S(1)}, u32[]{:S(2)}, u32[]{:S(2)}) collective-permute-start(s32[1024,32]{0,1:T(8,128)S(1)} %pad_add_fusion.1), channel_id=1, source_target_pairs={{0,8},{1,9},{2,10},{3,11},{4,12},{5,13},{6,14},{7,15},{8,0},{9,1},... | collective-permute-start | bytes 393224 | tf_op jit(solution)/shard_map/ppermute | solution.py:53
  54.6 1.5 %collective-permute-start.8 = (s32[1024,4]{0,1:T(4,128)S(1)}, s32[1024,4]{0,1:T(4,128)S(1)}, u32[]{:S(2)}, u32[]{:S(2)}) collective-permute-start(s32[1024,4]{0,1:T(4,128)S(1)} %get-tuple-element.14), channel_id=1, source_target_pairs={{0,15},{1,0},{2,1},{3,2},{4,3},{5,4},{6,5},{7,6},{8,7},{9,8},{10,9... | collective-permute-start | bytes 49160 | tf_op jit(solution)/shard_map/ppermute | solution.py:53
  56.1 5.1 %collective-permute-start.9 = (s32[1024,8]{0,1:T(8,128)S(1)}, s32[1024,8]{0,1:T(8,128)S(1)}, u32[]{:S(2)}, u32[]{:S(2)}) collective-permute-start(s32[1024,8]{0,1:T(8,128)S(1)} %pad_add_fusion.8), channel_id=1, source_target_pairs={{0,14},{1,15},{2,0},{3,1},{4,2},{5,3},{6,4},{7,5},{8,6},{9,7},{10,... | collective-permute-start | bytes 98312 | tf_op jit(solution)/shard_map/ppermute | solution.py:53
  61.3 8.4 %collective-permute-start.10 = (s32[1024,16]{0,1:T(8,128)S(1)}, s32[1024,16]{0,1:T(8,128)S(1)}, u32[]{:S(2)}, u32[]{:S(2)}) collective-permute-start(s32[1024,16]{0,1:T(8,128)S(1)} %pad_add_fusion.5), channel_id=1, source_target_pairs={{0,12},{1,13},{2,14},{3,15},{4,0},{5,1},{6,2},{7,3},{8,4},{9,5},{1... | collective-permute-start | bytes 196616 | tf_op jit(solution)/shard_map/ppermute | solution.py:53
  69.7 8.6 %collective-permute-start.11 = (s32[1024,32]{0,1:T(8,128)S(1)}, s32[1024,32]{0,1:T(8,128)S(1)}, u32[]{:S(2)}, u32[]{:S(2)}) collective-permute-start(s32[1024,32]{0,1:T(8,128)S(1)} %pad_add_fusion.2), channel_id=1, source_target_pairs={{0,8},{1,9},{2,10},{3,11},{4,12},{5,13},{6,14},{7,15},{8,0},{9,1},... | collective-permute-start | bytes 393224 | tf_op jit(solution)/shard_map/ppermute | solution.py:53
